TPU v7x, 128 devices: a 2x2x16 block of a 8x8x16 slice. The times are simulated.
128 devices in a mesh: groups: 4 (over y, x), seq: 16 (over z), sub: 2 (over core).
Axes of the slice: x: 2, y: 2, z: 16, core: 2. Of those that a mesh axis runs over, the one named last changes fastest.
The devices are a block of a 8x8x16 slice.
Arguments:
- query_proj: bfloat16 [8192, 4096], P(('groups', 'seq'), 'sub'), parts along dimension 0, may hold values from -2500 to 2500
- key_proj: bfloat16 [8192, 4096], P(('groups', 'seq'), 'sub'), parts along dimension 0, may hold values from -2500 to 2500
- value_proj: bfloat16 [8192, 4096], P(('groups', 'seq'), 'sub'), parts along dimension 0, may hold values from -12 to 12
- out_weight: bfloat16 [4096, 5120], P('sub', 'seq'), may hold values from -0.5 to 0.5
- query_gain: float32 [4096], P('sub'), may hold values from 0.25 to 1.75
- key_gain: float32 [4096], P('sub'), may hold values from 0.25 to 1.75
- gate_scale: float32 [20480], P(('groups', 'sub')), parts along dimension 0, may hold values from 0.5 to 2
- key_count: int32 [4], P('groups'), parts along dimension 0, may hold values from 1024 to 2048
Outputs:
- attended_out: bfloat16 [8192, 5120], P(('groups', 'seq'), 'sub'), parts along dimension 0
There are 4 independent parts, one for each index of `groups`. A program takes and returns all parts, laid end to end along the dimension named above; an argument that names none is the same for every part. Nothing has to cross between parts.
All inputs are finite; a program needn't handle non-finite values.
Results may differ from a plain program's by a relative error of at most 0.012.
Values may be sent and summed in bfloat16 or wider, within the bound.
A program may use at most 128 MiB of HBM per device.

v0:
```python
import math
import jax
import jax.numpy as jnp
from jax import lax
from jax.sharding import PartitionSpec as P

HD = 128
epsilon = 1e-06
key_block = 512


def gathered_total(array, axis):
    return lax.all_gather(array, axis).sum(0)


def cut_along(array, dim, size):
    shape = array.shape
    pieces = array.reshape(*shape[:dim], size, shape[dim] // size, *shape[dim + 1 :])
    return jnp.moveaxis(pieces, dim, 0)


def sent_and_summed(array, axis, dim):
    pieces = cut_along(array, dim, lax.axis_size(axis))
    arrived = lax.all_to_all(pieces, axis, split_axis=0, concat_axis=0, tiled=True)
    return arrived.astype(jnp.float32).sum(axis=0)


def fold_keys(running, queries, key_rows, value_rows, offset, live_keys):
    row_total = key_rows.shape[0]
    blocks = row_total // key_block
    head_count = queries.shape[1]
    key_blocks = key_rows.reshape(blocks, key_block, head_count, HD)
    value_blocks = value_rows.reshape(blocks, key_block, head_count, HD)
    scale = 1.0 / math.sqrt(HD)

    def one_block(running, element):
        key_piece, value_piece, block_index = element
        highest, weight_sum, accumulated = running
        scores = (
            jnp.einsum("qhd,khd->hqk", queries, key_piece, preferred_element_type=jnp.float32)
            * scale
        )
        positions = offset + block_index * key_block + jnp.arange(key_block)
        usable = (positions < live_keys)[None, None, :]
        scores = jnp.where(usable, scores, -1e30)
        newest = jnp.maximum(highest, jnp.max(scores, axis=2))
        shrink = jnp.exp(highest - newest)
        weights = jnp.where(usable, jnp.exp(scores - newest[:, :, None]), 0.0)
        weight_sum = weight_sum * shrink + jnp.sum(weights, axis=2)
        product = jnp.einsum(
            "hqk,khd->qhd",
            weights.astype(jnp.bfloat16),
            value_piece,
            preferred_element_type=jnp.float32,
        )
        accumulated = accumulated * shrink.T[:, :, None] + product
        return ((newest, weight_sum, accumulated), None)

    running, unused = lax.scan(one_block, running, (key_blocks, value_blocks, jnp.arange(blocks)))
    return running


def empty_state(query_rows, head_count):
    return (
        jnp.full((head_count, query_rows), -1e30, jnp.float32),
        jnp.zeros((head_count, query_rows), jnp.float32),
        jnp.zeros((query_rows, head_count, HD), jnp.float32),
    )


def finish(running):
    highest, weight_sum, accumulated = running
    result = accumulated / weight_sum.T[:, :, None]
    return result.reshape(result.shape[0], -1).astype(jnp.bfloat16)


def shards(
    query_proj, key_proj, value_proj, out_weight, query_gain, key_gain, gate_scale, key_count
):
    features = query_proj.shape[1]
    query_wide = query_proj.astype(jnp.float32)
    key_wide = key_proj.astype(jnp.float32)
    squares = (
        gathered_total(jnp.sum(query_wide * query_wide, axis=1), "sub"),
        gathered_total(jnp.sum(key_wide * key_wide, axis=1), "sub"),
    )
    all_features = features * lax.axis_size("sub")
    query_normed = (
        query_wide * lax.rsqrt(squares[0] / all_features + epsilon)[:, None] * query_gain
    ).astype(jnp.bfloat16)
    key_normed = (
        key_wide * lax.rsqrt(squares[1] / all_features + epsilon)[:, None] * key_gain
    ).astype(jnp.bfloat16)
    live_keys = key_count[0]
    query_all, key_all, value_all = (
        lax.all_to_all(query_normed, "seq", split_axis=1, concat_axis=0, tiled=True),
        lax.all_to_all(key_normed, "seq", split_axis=1, concat_axis=0, tiled=True),
        lax.all_to_all(value_proj, "seq", split_axis=1, concat_axis=0, tiled=True),
    )
    seq_rows = query_all.shape[0]
    head_count = query_all.shape[1] // HD
    running = fold_keys(
        empty_state(seq_rows, head_count),
        query_all.reshape(seq_rows, head_count, HD),
        key_all,
        value_all,
        0,
        live_keys,
    )
    attended = lax.all_to_all(finish(running), "seq", split_axis=0, concat_axis=1, tiled=True)
    partial_value = jnp.dot(
        attended,
        lax.all_gather(out_weight, "seq", axis=1, tiled=True),
        preferred_element_type=jnp.float32,
    )
    summed = sent_and_summed(partial_value.astype(jnp.bfloat16), "sub", 1)
    return (summed * gate_scale).astype(jnp.bfloat16)


def solution(mesh):
    placed = (
        P(("groups", "seq"), "sub"),
        P(("groups", "seq"), "sub"),
        P(("groups", "seq"), "sub"),
        P("sub", "seq"),
        P("sub"),
        P("sub"),
        P(("groups", "sub")),
        P("groups"),
    )
    return jax.shard_map(
        shards, mesh=mesh, in_specs=placed, out_specs=P(("groups", "seq"), "sub"), check_vma=False
    )
```

profile of v0, /device:TPU:69, one launch (start us, length us, event | category | flops | bytes accessed | tf_op | source)
XLA Modules:
  0.0 359.0 jit_solution(15972077560654113518)
XLA Ops:
  6.5 0.0 copy-start.1
  6.5 0.0 copy-start.4
  6.6 0.0 copy-start.2
  6.6 0.0 all-gather.6.cloned.1.call-start
  6.6 0.7 all-gather.6.cloned.1.call-update
  7.3 1.3 copy.24
  8.6 0.3 fusion.23
  8.9 11.4 %all-gather.2 = f32[2,1,128]{2,1,0:T(1,128)S(1)} all-gather(f32[1,1,128]{2,1,0:T(1,128)S(1)} %bitcast.88), channel_id=2, replica_groups=mesh['groups'=4,'seq'=16,'sub'=2] {'sub'}, dimensions={0}, use_global_device_ids=true | all-gather | bytes 1536 | tf_op jit(solution)/shard_map/all_gather | solution.py:13
  20.4 1.8 fusion.25
  22.2 8.3 %all-to-all-start = ((bf16[128,16,128]{0,2,1:T(8,128)(2,1)}), bf16[128,16,128]{0,2,1:T(8,128)(2,1)S(1)}, u32[]{:S(2)}, u32[]{:S(2)}) async-start(bf16[128,16,128]{0,2,1:T(8,128)(2,1)} %bitcast.2), calls=%async_computation | async-start | bytes 1048576 | tf_op jit(solution)/shard_map/all_to_all | solution.py:97
  30.5 0.0 copy-done.1
  30.5 0.3 copy.26
  30.8 0.3 fusion.26
  31.0 2.1 all-gather.3
  33.2 0.0 copy-done.4
  33.2 1.1 fusion.28
  34.4 26.8 %all-to-all-done = bf16[128,16,128]{0,2,1:T(8,128)(2,1)S(1)} async-done(((bf16[128,16,128]{0,2,1:T(8,128)(2,1)}), bf16[128,16,128]{0,2,1:T(8,128)(2,1)S(1)}, u32[]{:S(2)}, u32[]{:S(2)}) %all-to-all-start) | async-done | bytes 524320 | tf_op jit(solution)/shard_map/all_to_all | solution.py:97
  61.1 10.6 %all-to-all-start.1 = ((bf16[128,16,128]{0,2,1:T(8,128)(2,1)}), bf16[128,16,128]{0,2,1:T(8,128)(2,1)S(1)}, u32[]{:S(2)}, u32[]{:S(2)}) async-start(bf16[128,16,128]{0,2,1:T(8,128)(2,1)} %bitcast.7), calls=%async_computation.1 | async-start | bytes 1048576 | tf_op jit(solution)/shard_map/all_to_all | solution.py:96
  71.7 0.0 copy-done.2
  71.7 1.0 copy.28
  72.7 29.4 %all-to-all-done.1 = bf16[128,16,128]{0,2,1:T(8,128)(2,1)S(1)} async-done(((bf16[128,16,128]{0,2,1:T(8,128)(2,1)}), bf16[128,16,128]{0,2,1:T(8,128)(2,1)S(1)}, u32[]{:S(2)}, u32[]{:S(2)}) %all-to-all-start.1) | async-done | bytes 524320 | tf_op jit(solution)/shard_map/all_to_all | solution.py:96
  102.1 10.9 %all-to-all-start.2 = ((bf16[128,16,128]{0,2,1:T(8,128)(2,1)}), bf16[128,16,128]{0,2,1:T(8,128)(2,1)S(1)}, u32[]{:S(2)}, u32[]{:S(2)}) async-start(bf16[128,16,128]{0,2,1:T(8,128)(2,1)} %bitcast.10), calls=%async_computation.2 | async-start | bytes 1048576 | tf_op jit(solution)/shard_map/all_to_all | solution.py:98
  113.1 0.3 copy.25
  113.4 0.3 copy.27
  113.7 29.6 %all-to-all-done.2 = bf16[128,16,128]{0,2,1:T(8,128)(2,1)S(1)} async-done(((bf16[128,16,128]{0,2,1:T(8,128)(2,1)}), bf16[128,16,128]{0,2,1:T(8,128)(2,1)S(1)}, u32[]{:S(2)}, u32[]{:S(2)}) %all-to-all-start.2) | async-done | bytes 524320 | tf_op jit(solution)/shard_map/all_to_all | solution.py:98
  143.2 1.0 copy.29
  144.3 42.3 %while.15 = (s32[]{:T(128)}, f32[1,2048]{1,0:T(1,128)S(1)}, f32[1,2048]{1,0:T(1,128)S(1)}, f32[2048,1,128]{0,2,1:T(8,128)S(1)}, s32[4]{0:T(128)S(1)}, /*index=5*...) while((s32[]{:T(128)}, f32[1,2048]{1,0:T(1,128)S(1)}, ...), condition=%wide.region_7.8_spmd.clone, body=%wide.region_4.7_spmd.clone.sunk | while | flops 551300096 | bytes 32377536 | solution.py:59
  144.3 0.6 dynamic_slice.29
  145.5 0.7 add_compare_fusion.2
  146.2 2.7 fusion.40
  148.9 0.0 copy-start
  148.9 3.6 %fusion.42 = f32[2048]{0:T(1024)S(1)} fusion(f32[512,2048]{1,0:T(8,128)} %get-tuple-element.194, f32[2048]{0:T(1024)S(1)} %bitcast.74, pred[512]{0:T(512)(128)(4,1)S(1)} %add_compare_fusion.2), kind=kLoop, calls=%fused_computation.3.clone.1 | loop fusion | flops 5240832 | bytes 4211200 | tf_op jit(solution)/shard_map/while/body/eval_jaxpr/reduce_sum | solution.py:49
  152.6 0.0 copy-done
  152.6 2.2 fusion.44
  154.8 0.6 dynamic_slice.29
  156.1 0.7 add_compare_fusion.2
  156.7 2.7 fusion.40
  159.5 3.6 %fusion.42 = f32[2048]{0:T(1024)S(1)} fusion(f32[512,2048]{1,0:T(8,128)} %get-tuple-element.194, f32[2048]{0:T(1024)S(1)} %bitcast.74, pred[512]{0:T(512)(128)(4,1)S(1)} %add_compare_fusion.2), kind=kLoop, calls=%fused_computation.3.clone.1 | loop fusion | flops 5240832 | bytes 4211200 | tf_op jit(solution)/shard_map/while/body/eval_jaxpr/reduce_sum | solution.py:49
  163.1 0.0 copy-done
  163.1 2.2 fusion.44
  165.4 0.6 dynamic_slice.29
  166.6 0.7 add_compare_fusion.2
  167.3 2.7 fusion.40
  170.0 3.6 %fusion.42 = f32[2048]{0:T(1024)S(1)} fusion(f32[512,2048]{1,0:T(8,128)} %get-tuple-element.194, f32[2048]{0:T(1024)S(1)} %bitcast.74, pred[512]{0:T(512)(128)(4,1)S(1)} %add_compare_fusion.2), kind=kLoop, calls=%fused_computation.3.clone.1 | loop fusion | flops 5240832 | bytes 4211200 | tf_op jit(solution)/shard_map/while/body/eval_jaxpr/reduce_sum | solution.py:49
  173.7 0.0 copy-done
  173.7 2.2 fusion.44
  176.0 0.6 dynamic_slice.29
  177.2 0.7 add_compare_fusion.2
  177.9 2.7 fusion.40
  180.6 3.6 %fusion.42 = f32[2048]{0:T(1024)S(1)} fusion(f32[512,2048]{1,0:T(8,128)} %get-tuple-element.194, f32[2048]{0:T(1024)S(1)} %bitcast.74, pred[512]{0:T(512)(128)(4,1)S(1)} %add_compare_fusion.2), kind=kLoop, calls=%fused_computation.3.clone.1 | loop fusion | flops 5240832 | bytes 4211200 | tf_op jit(solution)/shard_map/while/body/eval_jaxpr/reduce_sum | solution.py:49
  184.3 0.0 copy-done
  184.3 2.2 fusion.44
  186.6 0.3 copy.32
  186.9 0.3 divide_convert_fusion
  187.2 41.0 %all_to_all.69 = bf16[16,128,128]{2,1,0:T(8,128)(2,1)S(1)} all-to-all(bf16[16,128,128]{2,1,0:T(8,128)(2,1)S(1)} %bitcast.78), channel_id=1, replica_groups=mesh['groups'=4,'seq'=16,'sub'=2] {'seq'}, dimensions={0} | all-to-all | bytes 1048576 | tf_op jit(solution)/shard_map/all_to_all | solution.py:110
  228.3 0.3 copy.33
  228.5 105.7 %all-gather.6.cloned.1.call-done = bf16[2048,5120]{0,1:T(8,128)(2,1)} async-done(((bf16[2048,320]{0,1:T(8,128)(2,1)}), bf16[2048,5120]{0,1:T(8,128)(2,1)}) %all-gather.6.cloned.1.call-update) | async-done | bytes 20971536 | tf_op jit(solution)/shard_map/all_gather | solution.py:113
  334.3 11.4 %convolution_convert_fusion = bf16[128,5120]{1,0:T(8,128)(2,1)S(1)} fusion(bf16[128,2048]{0,1:T(8,128)(2,1)S(1)} %bitcast.76, bf16[2048,5120]{0,1:T(8,128)(2,1)} %all-gather.6.cloned.1.call-done), kind=kOutput, calls=%fused_computation.30 | convolution fusion | flops 2685009920 | bytes 22806528 | tf_op jit(solution)/shard_map/dot_general | solution.py:111
  345.7 0.0 copy-start.3
  345.7 0.1 copy.37
  345.8 5.3 %all_to_all.70 = bf16[2,128,2560]{2,1,0:T(8,128)(2,1)S(1)} all-to-all(bf16[2,128,2560]{2,1,0:T(8,128)(2,1)S(1)} %bitcast.72), channel_id=1, replica_groups=mesh['groups'=4,'seq'=16,'sub'=2] {'sub'}, dimensions={0} | all-to-all | bytes 2621440 | tf_op jit(solution)/shard_map/all_to_all | solution.py:24
  351.1 0.2 convert_reduce_fusion
  351.3 0.0 copy-done.3
  351.3 0.9 multiply_convert_fusion
  (23 shorter events, 0.3 us)
Async XLA Ops:
  6.5 23.9 %copy-start.1 = (bf16[128,2048]{1,0:T(8,128)(2,1)S(1)}, bf16[128,2048]{1,0:T(8,128)(2,1)}, u32[]{:S(2)}) copy-start(bf16[128,2048]{1,0:T(8,128)(2,1)} %param.10) | copy-start | bytes 1572868
  6.5 26.7 %copy-start.4 = (f32[2048]{0:T(1024)S(1)}, f32[2048]{0:T(1024)}, u32[]{:S(2)}) copy-start(f32[2048]{0:T(1024)} %param.14) | copy-start | bytes 24580
  6.6 65.2 %copy-start.2 = (bf16[128,2048]{1,0:T(8,128)(2,1)S(1)}, bf16[128,2048]{1,0:T(8,128)(2,1)}, u32[]{:S(2)}) copy-start(bf16[128,2048]{1,0:T(8,128)(2,1)} %param.12) | copy-start | bytes 1572868
  6.6 327.7 %all-gather.6.cloned.1.call-start = ((), (), s32[]{:S(2)}) async-start(), calls=%async_computation.5 | async-start | bytes 22282240 | tf_op jit(solution)/shard_map/all_gather | solution.py:113
  22.2 39.0 %all-to-all-start = ((bf16[128,16,128]{0,2,1:T(8,128)(2,1)}), bf16[128,16,128]{0,2,1:T(8,128)(2,1)S(1)}, u32[]{:S(2)}, u32[]{:S(2)}) async-start(bf16[128,16,128]{0,2,1:T(8,128)(2,1)} %bitcast.2), calls=%async_computation | async-start | bytes 1048576 | tf_op jit(solution)/shard_map/all_to_all | solution.py:97
  61.1 41.0 %all-to-all-start.1 = ((bf16[128,16,128]{0,2,1:T(8,128)(2,1)}), bf16[128,16,128]{0,2,1:T(8,128)(2,1)S(1)}, u32[]{:S(2)}, u32[]{:S(2)}) async-start(bf16[128,16,128]{0,2,1:T(8,128)(2,1)} %bitcast.7), calls=%async_computation.1 | async-start | bytes 1048576 | tf_op jit(solution)/shard_map/all_to_all | solution.py:96
  102.1 41.1 %all-to-all-start.2 = ((bf16[128,16,128]{0,2,1:T(8,128)(2,1)}), bf16[128,16,128]{0,2,1:T(8,128)(2,1)S(1)}, u32[]{:S(2)}, u32[]{:S(2)}) async-start(bf16[128,16,128]{0,2,1:T(8,128)(2,1)} %bitcast.10), calls=%async_computation.2 | async-start | bytes 1048576 | tf_op jit(solution)/shard_map/all_to_all | solution.py:98
  148.9 3.7 %copy-start = (f32[512,2048]{1,0:T(8,128)S(1)}, f32[512,2048]{1,0:T(8,128)}, u32[]{:S(2)}) copy-start(f32[512,2048]{1,0:T(8,128)} %get-tuple-element.194) | copy-start | bytes 12582916 | tf_op jit(solution)/shard_map/while
  159.4 3.7 %copy-start = (f32[512,2048]{1,0:T(8,128)S(1)}, f32[512,2048]{1,0:T(8,128)}, u32[]{:S(2)}) copy-start(f32[512,2048]{1,0:T(8,128)} %get-tuple-element.194) | copy-start | bytes 12582916 | tf_op jit(solution)/shard_map/while
  170.0 3.7 %copy-start = (f32[512,2048]{1,0:T(8,128)S(1)}, f32[512,2048]{1,0:T(8,128)}, u32[]{:S(2)}) copy-start(f32[512,2048]{1,0:T(8,128)} %get-tuple-element.194) | copy-start | bytes 12582916 | tf_op jit(solution)/shard_map/while
  180.6 3.7 %copy-start = (f32[512,2048]{1,0:T(8,128)S(1)}, f32[512,2048]{1,0:T(8,128)}, u32[]{:S(2)}) copy-start(f32[512,2048]{1,0:T(8,128)} %get-tuple-element.194) | copy-start | bytes 12582916 | tf_op jit(solution)/shard_map/while
  345.7 5.6 %copy-start.3 = (f32[2560]{0:T(1024)S(1)}, f32[2560]{0:T(1024)}, u32[]{:S(2)}) copy-start(f32[2560]{0:T(1024)} %param.16) | copy-start | bytes 30724
Sparse Core Ops, SparseCore 0:
  9.0 325.2 all-gather.5
where the time goes:
time: 360 us; the launch traced here: 359 us
  waiting for transfers between devices  192 us (53%)
  blocking collectives  59.8 us (17%)
  matrix products  31.2 us (9%)
  starting transfers between devices  29.8 us (8%)
  other arithmetic  22.4 us (6%)
  between operations  13.6 us (4%)
  local copies, waits for them, and re-layouts  7.39 us (2%)
    all_gather x1, waiting for transfers between devices, shards(): lax.all_gather(out_weight, 'seq', axis=1, tiled=True)  106 us
    all_to_all x1, blocking collectives, shards(): lax.all_to_all(finish(running), 'seq', split_axis=0, concat_axis=1, tiled...  41 us
    all_to_all x1, waiting for transfers between devices, shards(): lax.all_to_all(value_proj, 'seq', split_axis=1, concat_axis=0, tiled=True)  29.6 us
    all_to_all x1, waiting for transfers between devices, shards(): lax.all_to_all(query_normed, 'seq', split_axis=1, concat_axis=0, tiled=True)  29.4 us
    all_to_all x1, waiting for transfers between devices, shards(): lax.all_to_all(key_normed, 'seq', split_axis=1, concat_axis=0, tiled=True)  26.8 us
    reduce_sum x4, other arithmetic, one_block(): weight_sum = weight_sum * shrink + jnp.sum(weights, axis=2)  14.5 us
    all_gather x2, blocking collectives, gathered_total(): return lax.all_gather(array, axis).sum(0)  13.5 us
    dot_general x1, matrix products, shards(): jnp.dot(attended, lax.all_gather(out_weight, 'seq', axis=1, tiled=True),...  11.4 us
  transfers between devices with their start and end apart: 4, of which 4 were waited for; matrix products, arithmetic and copies ran while one was open for 13% of the time, Pallas kernels for 0%

commit v1 on v0

--- a/solution.py
+++ b/solution.py
@@ -110,7 +110,9 @@
     attended = lax.all_to_all(finish(running), "seq", split_axis=0, concat_axis=1, tiled=True)
     partial_value = jnp.dot(
         attended,
-        lax.all_gather(out_weight, "seq", axis=1, tiled=True),
+        jnp.concatenate(
+            lax.all_to_all(jnp.stack([out_weight] * lax.axis_size("seq")), "seq", 0, 0), axis=1
+        ),
         preferred_element_type=jnp.float32,
     )
     summed = sent_and_summed(partial_value.astype(jnp.bfloat16), "sub", 1)

time: 360 us -> 1120 us (3.11)
  waiting for transfers between devices: 192 us -> 962 us
  starting transfers between devices: 29.8 us -> 47.1 us
  between operations: 13.6 us -> 0.19 us
  matrix products: 31.2 us -> 19.7 us
    all_to_all x0 -> x1, waiting for transfers between devices: none -> 900 us  [shards(): lax.all_to_all(jnp.stack([out_weight] * lax.axis_size('seq')), 'seq', 0, 0)]
    all_gather x1 -> x0, waiting for transfers between devices: 106 us -> none  [shards(): lax.all_gather(out_weight, 'seq', axis=1, tiled=True)]
    all_to_all x0 -> x1, starting transfers between devices: none -> 12.9 us  [shards(): lax.all_to_all(jnp.stack([out_weight] * lax.axis_size('seq')), 'seq', 0, 0)]
    all_to_all x1, waiting for transfers between devices: 29.4 us -> 17.6 us  [shards(): lax.all_to_all(query_normed, 'seq', split_axis=1, concat_axis=0, tiled=True)]
  transfers between devices with their start and end apart: 4 -> 4, of which waited for: 4 -> 4; matrix products, arithmetic and copies ran while one was open for 13% -> 0% of each run, Pallas kernels for 0% -> 0%
where the time goes in v1:
time: 1120 us; the launch traced here: 1110 us
  waiting for transfers between devices  962 us (86%)
  blocking collectives  54.8 us (5%)
  starting transfers between devices  47.1 us (4%)
  matrix products  19.7 us (2%)
  local copies, waits for them, and re-layouts  15.3 us (1%)
  other arithmetic  13 us (1%)
    all_to_all x1, waiting for transfers between devices, shards(): lax.all_to_all(jnp.stack([out_weight] * lax.axis_size('seq')), 'seq', 0, 0)  900 us
    all_to_all x1, blocking collectives, shards(): lax.all_to_all(finish(running), 'seq', split_axis=0, concat_axis=1, tiled...  35.4 us
  transfers between devices with their start and end apart: 4, of which 4 were waited for; matrix products, arithmetic and copies ran while one was open for 0% of the time, Pallas kernels for 0%

profile of v1, /device:TPU:69, one launch (start us, length us, event | category | flops | bytes accessed | tf_op | source)
XLA Modules:
  0.0 1114.9 jit_solution(8410578874869810362)
XLA Ops:
  0.0 0.0 copy-start.3
  0.0 0.0 copy-start.1
  0.0 1.4 copy.27
  1.4 0.3 fusion.26
  1.7 11.4 %all-gather.3 = f32[2,1,128]{2,1,0:T(1,128)S(1)} all-gather(f32[1,1,128]{2,1,0:T(1,128)S(1)} %bitcast.91), channel_id=3, replica_groups=mesh['groups'=4,'seq'=16,'sub'=2] {'sub'}, dimensions={0}, use_global_device_ids=true | all-gather | bytes 1536 | tf_op jit(solution)/shard_map/all_gather | solution.py:13
  13.1 1.8 fusion.28
  14.9 8.3 all-to-all-start.1
  23.2 1.3 copy.25
  24.5 0.3 fusion.23
  24.8 2.1 all-gather.2
  27.0 0.0 copy-done.3
  27.0 1.1 fusion.25
  28.1 17.6 %all-to-all-done.1 = bf16[128,16,128]{0,2,1:T(8,128)(2,1)S(1)} async-done(((bf16[128,16,128]{0,2,1:T(8,128)(2,1)}), bf16[128,16,128]{0,2,1:T(8,128)(2,1)S(1)}, u32[]{:S(2)}, u32[]{:S(2)}) %all-to-all-start.1) | async-done | bytes 524320 | tf_op jit(solution)/shard_map/all_to_all | solution.py:96
  45.7 13.1 %all-to-all-start = ((bf16[128,16,128]{0,2,1:T(8,128)(2,1)}), bf16[128,16,128]{0,2,1:T(8,128)(2,1)S(1)}, u32[]{:S(2)}, u32[]{:S(2)}) async-start(bf16[128,16,128]{0,2,1:T(8,128)(2,1)} %bitcast.2), calls=%async_computation | async-start | bytes 1048576 | tf_op jit(solution)/shard_map/all_to_all | solution.py:97
  58.8 0.0 copy-done.1
  58.8 1.0 copy.29
  59.8 21.7 %all-to-all-done = bf16[128,16,128]{0,2,1:T(8,128)(2,1)S(1)} async-done(((bf16[128,16,128]{0,2,1:T(8,128)(2,1)}), bf16[128,16,128]{0,2,1:T(8,128)(2,1)S(1)}, u32[]{:S(2)}, u32[]{:S(2)}) %all-to-all-start) | async-done | bytes 524320 | tf_op jit(solution)/shard_map/all_to_all | solution.py:97
  81.5 12.8 %all-to-all-start.2 = ((bf16[128,16,128]{0,2,1:T(8,128)(2,1)}), bf16[128,16,128]{0,2,1:T(8,128)(2,1)S(1)}, u32[]{:S(2)}, u32[]{:S(2)}) async-start(bf16[128,16,128]{0,2,1:T(8,128)(2,1)} %bitcast.10), calls=%async_computation.2 | async-start | bytes 1048576 | tf_op jit(solution)/shard_map/all_to_all | solution.py:98
  94.4 0.3 copy.28
  94.7 0.3 copy.26
  95.0 22.1 %all-to-all-done.2 = bf16[128,16,128]{0,2,1:T(8,128)(2,1)S(1)} async-done(((bf16[128,16,128]{0,2,1:T(8,128)(2,1)}), bf16[128,16,128]{0,2,1:T(8,128)(2,1)S(1)}, u32[]{:S(2)}, u32[]{:S(2)}) %all-to-all-start.2) | async-done | bytes 524320 | tf_op jit(solution)/shard_map/all_to_all | solution.py:98
  117.1 0.3 copy.30
  117.4 22.0 %while.15 = (s32[]{:T(128)}, f32[1,2048]{1,0:T(1,128)S(1)}, f32[1,2048]{1,0:T(1,128)S(1)}, f32[2048,1,128]{0,2,1:T(8,128)S(1)}, s32[4]{0:T(128)S(1)}, /*index=5*...) while((s32[]{:T(128)}, f32[1,2048]{1,0:T(1,128)S(1)}, ...), condition=%wide.region_7.8_spmd.clone, body=%wide.region_4.7_spmd.clone.sunk | while | flops 551300096 | bytes 15599793 | solution.py:59
  117.4 0.7 dynamic_slice.29
  118.8 0.7 add_compare_fusion.2
  119.4 0.8 fusion.40
  120.2 1.3 fusion.42
  121.6 1.3 fusion.44
  122.9 0.7 dynamic_slice.29
  124.3 0.7 add_compare_fusion.2
  124.9 0.8 fusion.40
  125.7 1.3 fusion.42
  127.1 1.3 fusion.44
  128.4 0.7 dynamic_slice.29
  129.8 0.7 add_compare_fusion.2
  130.4 0.8 fusion.40
  131.2 1.3 fusion.42
  132.6 1.3 fusion.44
  133.9 0.7 dynamic_slice.29
  135.3 0.7 add_compare_fusion.2
  135.9 0.8 fusion.40
  136.7 1.3 fusion.42
  138.1 1.3 fusion.44
  139.4 0.0 copy-start
  139.4 0.3 copy.33
  139.8 0.3 divide_convert_fusion
  140.1 35.4 %all_to_all.74 = bf16[16,128,128]{2,1,0:T(8,128)(2,1)S(1)} all-to-all(bf16[16,128,128]{2,1,0:T(8,128)(2,1)S(1)} %bitcast.81), channel_id=1, replica_groups=mesh['groups'=4,'seq'=16,'sub'=2] {'seq'}, dimensions={0} | all-to-all | bytes 1048576 | tf_op jit(solution)/shard_map/all_to_all | solution.py:110
  175.5 0.0 copy-done
  175.5 7.3 stack.2
  182.8 12.9 %all-to-all-start.4 = ((bf16[16,2048,320]{1,2,0:T(8,128)(2,1)}), bf16[16,2048,320]{1,2,0:T(8,128)(2,1)}, u32[]{:S(2)}, u32[]{:S(2)}) async-start(bf16[16,2048,320]{1,2,0:T(8,128)(2,1)} %stack.2), calls=%async_computation.4 | async-start | bytes 41943040 | tf_op jit(solution)/shard_map/all_to_all | solution.py:114
  195.7 0.3 copy.34
  196.0 900.4 %all-to-all-done.4 = bf16[16,2048,320]{1,2,0:T(8,128)(2,1)} async-done(((bf16[16,2048,320]{1,2,0:T(8,128)(2,1)}), bf16[16,2048,320]{1,2,0:T(8,128)(2,1)}, u32[]{:S(2)}, u32[]{:S(2)}) %all-to-all-start.4) | async-done | bytes 20971552 | tf_op jit(solution)/shard_map/all_to_all | solution.py:114
  1096.4 11.4 %convolution_convert_fusion = bf16[128,5120]{1,0:T(8,128)(2,1)S(1)} fusion(bf16[128,2048]{0,1:T(8,128)(2,1)S(1)} %bitcast.79, bf16[2048,5120]{0,1:T(8,128)(2,1)} %bitcast.19), kind=kOutput, calls=%fused_computation.30 | convolution fusion | flops 2685009920 | bytes 22806528 | tf_op jit(solution)/shard_map/dot_general | solution.py:111
  1107.8 0.0 copy-start.2
  1107.8 0.1 copy.38
  1107.9 5.8 all_to_all.75
  1113.8 0.2 convert_reduce_fusion
  1114.0 0.0 copy-done.2
  1114.0 0.9 multiply_convert_fusion
  (20 shorter events, 0.3 us)
Async XLA Ops:
  0.0 27.0 %copy-start.3 = (f32[2048]{0:T(1024)S(1)}, f32[2048]{0:T(1024)}, u32[]{:S(2)}) copy-start(f32[2048]{0:T(1024)} %param.15) | copy-start | bytes 24580
  0.0 58.8 %copy-start.1 = (bf16[128,2048]{1,0:T(8,128)(2,1)S(1)}, bf16[128,2048]{1,0:T(8,128)(2,1)}, u32[]{:S(2)}) copy-start(bf16[128,2048]{1,0:T(8,128)(2,1)} %param.12) | copy-start | bytes 1572868
  14.9 30.8 %all-to-all-start.1 = ((bf16[128,16,128]{0,2,1:T(8,128)(2,1)}), bf16[128,16,128]{0,2,1:T(8,128)(2,1)S(1)}, u32[]{:S(2)}, u32[]{:S(2)}) async-start(bf16[128,16,128]{0,2,1:T(8,128)(2,1)} %bitcast.7), calls=%async_computation.1 | async-start | bytes 1048576 | tf_op jit(solution)/shard_map/all_to_all | solution.py:96
  45.7 35.8 %all-to-all-start = ((bf16[128,16,128]{0,2,1:T(8,128)(2,1)}), bf16[128,16,128]{0,2,1:T(8,128)(2,1)S(1)}, u32[]{:S(2)}, u32[]{:S(2)}) async-start(bf16[128,16,128]{0,2,1:T(8,128)(2,1)} %bitcast.2), calls=%async_computation | async-start | bytes 1048576 | tf_op jit(solution)/shard_map/all_to_all | solution.py:97
  81.5 35.6 %all-to-all-start.2 = ((bf16[128,16,128]{0,2,1:T(8,128)(2,1)}), bf16[128,16,128]{0,2,1:T(8,128)(2,1)S(1)}, u32[]{:S(2)}, u32[]{:S(2)}) async-start(bf16[128,16,128]{0,2,1:T(8,128)(2,1)} %bitcast.10), calls=%async_computation.2 | async-start | bytes 1048576 | tf_op jit(solution)/shard_map/all_to_all | solution.py:98
  139.4 36.1 %copy-start = (bf16[2048,320]{0,1:T(8,128)(2,1)S(1)}, bf16[2048,320]{0,1:T(8,128)(2,1)}, u32[]{:S(2)}) copy-start(bf16[2048,320]{0,1:T(8,128)(2,1)} %param.13) | copy-start | bytes 3932164
  182.8 913.6 %all-to-all-start.4 = ((bf16[16,2048,320]{1,2,0:T(8,128)(2,1)}), bf16[16,2048,320]{1,2,0:T(8,128)(2,1)}, u32[]{:S(2)}, u32[]{:S(2)}) async-start(bf16[16,2048,320]{1,2,0:T(8,128)(2,1)} %stack.2), calls=%async_computation.4 | async-start | bytes 41943040 | tf_op jit(solution)/shard_map/all_to_all | solution.py:114
  1107.8 6.1 copy-start.2
